TPU v7x, 32 devices: a whole 2x2x4 slice. The times are simulated.
32 devices in a mesh: src: 4 (over y, x), col: 8 (over z, core).
Axes of the slice: x: 2, y: 2, z: 4, core: 2. Of those that a mesh axis runs over, the one named last changes fastest.
Arguments:
- saved_tables: float32 [4, 16384, 256], P('src', 'col'), may hold values from -6 to 6
- saved_state: float32 [4, 16384], P('src', 'col'), may hold values from 0.05 to 4
- slot_table: int32 [4], replicated, may hold values from 0 to 3, each once
- row_ids: int32 [4, 2048], replicated, may hold values from 0 to 16383
- grads: float32 [4, 256, 2048], P('src', 'col'), may hold values from -6 to 6
Outputs:
- tables_out: float32 [4, 256, 16384], P('src', 'col')
- state_out: float32 [4, 16384], P('src')
Inputs may be any that keep to these rules, and one draw needn't show every extreme that they name: `slot_table`: each table is in exactly one slot. `row_ids`: row ids may repeat.
All inputs are finite; a program needn't handle non-finite values.
Results may differ from a plain program's by a relative error of at most 0.00002.
Values sent between devices are 32-bit elements; how exact they have to be, the bound alone decides.
A program may use at most 192 MiB of HBM per device.

v0:
```python
import jax
import jax.numpy as jnp
from jax import lax
from jax.sharding import PartitionSpec as P

D = 256


learn_rate = 0.5
epsilon = 1e-08


def reshard(tables, state):
    by_columns = lax.all_to_all(tables, "col", split_axis=2, concat_axis=1, tiled=True)
    state_full = lax.all_gather(state, "col", axis=1, tiled=True)
    return (by_columns, state_full)


def slot_inputs(slot_table, row_ids, every_grad):
    table = slot_table[lax.axis_index("src")]
    slot_ids = lax.dynamic_index_in_dim(row_ids, table, 0, keepdims=False)
    slot_grad = lax.dynamic_index_in_dim(every_grad, table, 0, keepdims=False)
    return (slot_ids, slot_grad)


def target_update(saved_tables, saved_state, slot_table, row_ids, grads):
    tables, state = reshard(saved_tables, saved_state)
    length = tables.shape[1]
    every_grad = lax.all_gather(grads, "src", axis=0, tiled=True)
    slot_ids, slot_grad = slot_inputs(slot_table, row_ids, every_grad)
    summed = jnp.zeros((length, slot_grad.shape[0]), jnp.float32).at[slot_ids].add(slot_grad.T)
    partial_value = jnp.sum(summed * summed, axis=1)
    total = lax.psum(partial_value, "col")
    new_state = state[0] + total / D
    new_tables = tables[0] - learn_rate * summed / (jnp.sqrt(new_state)[:, None] + epsilon)
    return (new_tables.T[None], new_state[None])


def body(saved_tables, saved_state, slot_table, row_ids, grads):
    return target_update(saved_tables, saved_state, slot_table, row_ids, grads)


def solution(mesh):
    placed = (P("src", "col", None), P("src", "col"), P(), P(), P("src", "col", None))
    return jax.shard_map(
        body,
        mesh=mesh,
        in_specs=placed,
        out_specs=(P("src", "col", None), P("src", None)),
        check_vma=False,
    )
```

profile of v0, /device:TPU:0, one launch (start us, length us, event | category | flops | bytes accessed | tf_op | source)
XLA Modules:
  0.0 161.8 jit_solution(5064605721100935365)
XLA Ops:
  7.2 0.0 copy-start.1
  7.2 6.0 %copy.13 = f32[1,2048,256]{1,0,2:T(1,128)} copy(f32[1,2048,256]{2,1,0:T(8,128)} %param.5) | data formatting | bytes 4194304 | tf_op args[0]
  13.2 6.4 %all-to-all-start = ((f32[1,2048,256]{1,0,2:T(1,128)}), f32[1,2048,256]{1,0,2:T(1,128)}, u32[]{:S(2)}, u32[]{:S(2)}) async-start(f32[1,2048,256]{1,0,2:T(1,128)} %copy.13), calls=%async_computation | async-start | bytes 4194304 | tf_op jit(solution)/shard_map/all_to_all | solution.py:14
  19.6 0.0 all-gather.2.cloned.1.call-start
  19.6 0.7 all-gather.2.cloned.1.call-update
  20.3 0.0 all-reduce.2.cloned.1.call-start
  20.3 0.0 copy-done.1
  20.4 0.6 dynamic_slice.11
  22.9 0.8 compare_select_fusion
  23.7 26.5 %all-gather.2.cloned.1.call-done = f32[4,32,2048]{2,1,0:T(8,128)} async-done(((f32[1,32,2048]{2,1,0:T(8,128)}), f32[4,32,2048]{2,1,0:T(8,128)}) %all-gather.2.cloned.1.call-update) | async-done | bytes 1048592 | tf_op jit(solution)/shard_map/all_gather | solution.py:29
  50.2 1.0 dynamic-slice_bitcast_fusion
  51.2 0.3 copy.15
  51.5 0.0 copy-start
  51.5 15.2 %scatter_custom_fusion = f32[16384,32]{1,0:T(8,128)} fusion(s32[2048]{0:T(1024)S(1)} %bitcast.22, f32[2048,32]{1,0:T(8,128)S(1)} %copy.15, f32[]{:T(128)} %constant.8.clone.1), kind=kCustom, calls=%fused_computation.3 | custom fusion | flops 65536 | bytes 2097156 | tf_op jit(solution)/shard_map/scatter-add | solution.py:31
  66.7 5.3 %multiply_reduce_fusion = f32[16384]{0:T(1024)} fusion(f32[16384,32]{1,0:T(8,128)} %scatter_custom_fusion), kind=kLoop, calls=%fused_computation.2 | loop fusion | flops 1032192 | bytes 2162688 | tf_op jit(solution)/shard_map/reduce_sum | solution.py:32
  72.0 0.0 all-reduce.2.cloned.1.call-update
  72.0 0.0 copy-done
  72.0 14.0 %all_gather.7 = f32[1,16384]{1,0:T(1,128)S(1)} all-gather(f32[1,2048]{1,0:T(1,128)S(1)} %copy-done), channel_id=1, replica_groups=mesh['src'=4,'col'=8] {'col'}, dimensions={1}, use_global_device_ids=true | all-gather | bytes 73728 | tf_op jit(solution)/shard_map/all_gather | solution.py:15
  86.0 40.8 %all-reduce.2.cloned.1.call-done = f32[16384]{0:T(1024)} async-done(((f32[16384]{0:T(1024)}), f32[16384]{0:T(1024)}) %all-reduce.2.cloned.1.call-update) | async-done | bytes 65552 | tf_op jit(solution)/shard_map/psum | solution.py:33
  126.8 1.5 sqrt_add_fusion
  128.3 0.0 all-to-all-done
  128.3 2.5 %copy.17 = f32[1,2048,256]{1,2,0:T(8,128)S(1)} copy(f32[1,2048,256]{1,0,2:T(1,128)} %all-to-all-done) | data formatting | bytes 4194304
  130.8 4.7 %copy.14 = f32[1,8,2048,32]{3,2,1,0:T(8,128)} copy(f32[1,8,2048,32]{2,3,1,0:T(8,128)S(1)} %bitcast.19) | data formatting | bytes 4194304 | tf_op jit(solution)/shard_map/all_to_all | solution.py:14
  135.4 13.3 %bitcast_subtract_fusion = f32[16384,32]{1,0:T(8,128)} fusion(f32[1,8,2048,32]{3,2,1,0:T(8,128)} %copy.14, f32[16384,32]{1,0:T(8,128)} %scatter_custom_fusion, f32[16384]{0:T(1024)S(1)} %get-tuple-element.8), kind=kLoop, calls=%fused_computation.1 | loop fusion | flops 1572864 | bytes 6356992 | tf_op jit(solution)/shard_map/sub | solution.py:35
  148.7 6.2 %copy.16 = f32[1,32,16384]{2,1,0:T(8,128)} copy(f32[1,32,16384]{1,2,0:T(8,128)} %bitcast.18) | data formatting | bytes 4194304
Async XLA Ops:
  7.2 13.2 %copy-start.1 = (s32[4]{0:T(128)S(1)}, s32[4]{0:T(128)}, u32[]{:S(2)}) copy-start(s32[4]{0:T(128)} %param.7) | copy-start | bytes 52
  13.2 115.1 %all-to-all-start = ((f32[1,2048,256]{1,0,2:T(1,128)}), f32[1,2048,256]{1,0,2:T(1,128)}, u32[]{:S(2)}, u32[]{:S(2)}) async-start(f32[1,2048,256]{1,0,2:T(1,128)} %copy.13), calls=%async_computation | async-start | bytes 4194304 | tf_op jit(solution)/shard_map/all_to_all | solution.py:14
  19.6 30.6 %all-gather.2.cloned.1.call-start = ((), (), s32[]{:S(2)}) async-start(), calls=%async_computation.1 | async-start | bytes 1310720 | tf_op jit(solution)/shard_map/all_gather | solution.py:29
  20.3 106.5 %all-reduce.2.cloned.1.call-start = ((), (), s32[]{:S(2)}) async-start(), calls=%async_computation.2 | async-start | bytes 131072 | tf_op jit(solution)/shard_map/psum | solution.py:33
  51.5 20.5 %copy-start = (f32[1,2048]{1,0:T(1,128)S(1)}, f32[1,2048]{1,0:T(1,128)}, u32[]{:S(2)}) copy-start(f32[1,2048]{1,0:T(1,128)} %param.6) | copy-start | bytes 24580
Sparse Core Ops, SparseCore 0:
  22.2 27.9 all-gather.1
  72.1 54.6 all-reduce.1
where the time goes:
time: 162 us
  waiting for transfers between devices  68.1 us (42%)
  other arithmetic  36 us (22%)
  local copies, waits for them, and re-layouts  21.3 us (13%)
  between operations  16 us (10%)
  blocking collectives  14 us (9%)
  starting transfers between devices  6.43 us (4%)
    psum x1, waiting for transfers between devices, target_update(): total = lax.psum(partial_value, 'col')  40.8 us
    all_gather x1, waiting for transfers between devices, target_update(): every_grad = lax.all_gather(grads, 'src', axis=0, tiled=True)  26.5 us
    scatter-add x1, other arithmetic, target_update(): jnp.zeros((length, slot_grad.shape[0]), jnp.float32).at[slot_ids]  15.2 us
    unnamed x7, local copies, waits for them, and re-layouts  14.8 us
    all_gather x1, blocking collectives, reshard(): state_full = lax.all_gather(state, 'col', axis=1, tiled=True)  14 us
    sub x1, other arithmetic, target_update(): tables[0] - learn_rate * summed / (jnp.sqrt(new_state)[:, None] + epsilon)  13.3 us
    all_to_all x1, starting transfers between devices, reshard(): lax.all_to_all(tables, 'col', split_axis=2, concat_axis=1, tiled=True)  6.35 us
    reduce_sum x1, other arithmetic, target_update(): partial_value = jnp.sum(summed * summed, axis=1)  5.25 us
  transfers between devices with their start and end apart: 3, of which 2 were waited for; matrix products, arithmetic and copies ran while one was open for 15% of the time, Pallas kernels for 0%

commit v1 on v0

v1 whole, which is shorter than its diff:
```python
import functools

import jax
import jax.numpy as jnp
from jax import lax
from jax.experimental import pallas as pl
from jax.experimental.pallas import tpu as pltpu
from jax.sharding import PartitionSpec as P

learn_rate = 0.5
epsilon = 1e-08

MESH = pl.DeviceIdType.MESH
LANES = 128
LOW = 256
GROUP = 4
CHUNKS = 4


def kernel(ns, nc, tab, state, slot_table, ids, grads, out, state_out,
           x, xt, tb, summed, gbuf, parts, hib, onehot, sq, rs, stbuf,
           x_sem, g_sem, gs_send, gs_recv, t_send, t_recv,
           q_send, q_recv, s_send, s_recv, o_sem):
    k = lax.axis_index("src")
    d = lax.axis_index("col")
    rows, width = x.shape
    cols, upd = gbuf.shape[1], gbuf.shape[2]
    total_rows = tb.shape[1]
    per = LANES // cols
    ch = rows // CHUNKS

    loads = []
    for c in range(CHUNKS):
        span = pl.ds(c * ch, ch)
        load = pltpu.make_async_copy(tab.at[0, span], x.at[span], x_sem.at[c])
        load.start()
        loads.append(load)
    own_grad = pltpu.make_async_copy(grads.at[0], gbuf.at[k], g_sem)
    own_grad.start()

    barrier = pltpu.get_barrier_semaphore()
    for m in range(1, nc):
        pl.semaphore_signal(barrier, inc=1, device_id=(k, d ^ m), device_id_type=MESH)
    for m in range(1, ns):
        pl.semaphore_signal(barrier, inc=1, device_id=(k ^ m, d), device_id_type=MESH)
    pl.semaphore_wait(barrier, nc + ns - 2)

    def grad_copy(m, owner):
        return pltpu.make_async_remote_copy(
            src_ref=grads.at[0], dst_ref=gbuf.at[owner],
            send_sem=gs_send.at[m], recv_sem=gs_recv.at[owner],
            device_id=(k ^ m, d), device_id_type=MESH)

    for m in range(1, ns):
        grad_copy(m, k).start()

    def table_copy(m, c, owner):
        e = d ^ m
        return pltpu.make_async_remote_copy(
            src_ref=xt.at[pl.ds(pl.multiple_of(e * cols, cols), cols), pl.ds(c * ch, ch)],
            dst_ref=tb.at[:, pl.ds(pl.multiple_of(owner * rows + c * ch, ch), ch)],
            send_sem=t_send.at[m, c], recv_sem=t_recv.at[owner, c],
            device_id=(k, e), device_id_type=MESH)

    own_half = d // per
    near = list(range(per - 1, 1, -1))
    far = list(range(nc - 1, per - 1, -1))

    def turn(half, c):
        at = pl.ds(pl.multiple_of(half * LANES, LANES), LANES)
        xt[at, pl.ds(c * ch, ch)] = x[pl.ds(c * ch, ch), at].T

    queue = []
    for c in range(CHUNKS):
        loads[c].wait()
        turn(own_half, c)
        for m in queue:
            table_copy(m, c - 1, d).start()
        queue = near
    for c in range(CHUNKS):
        for h in range(1, width // LANES):
            turn(own_half ^ h, c)
        if c == 0:
            for m in near:
                table_copy(m, CHUNKS - 1, d).start()
        else:
            for m in far:
                table_copy(m, c - 1, d).start()

    t = slot_table[k]
    row = ids[pl.ds(t, 1), :]
    low = jnp.bitwise_and(row, LOW - 1).astype(jnp.float32)
    lane = lax.broadcasted_iota(jnp.int32, (LANES, LANES), 1).astype(jnp.float32)
    for b in range(upd // LANES):
        column = jnp.broadcast_to(low[:, b * LANES:(b + 1) * LANES], (LANES, LANES)).T
        for w in range(LOW // LANES):
            onehot[b * LANES:(b + 1) * LANES, w * LANES:(w + 1) * LANES] = jnp.where(
                column == lane + float(w * LANES), 1.0, 0.0).astype(jnp.bfloat16)
    for m in far:
        table_copy(m, CHUNKS - 1, d).start()
    for c in range(CHUNKS):
        table_copy(1, c, d).start()
    high = (row // LOW).astype(jnp.float32)
    hib[...] = jnp.broadcast_to(high, hib.shape).astype(jnp.bfloat16)

    own_grad.wait()
    for m in range(1, ns):
        grad_copy(m, k ^ m).wait_recv()
    g = gbuf[t]
    first = g.astype(jnp.bfloat16)
    rest = g - first.astype(jnp.float32)
    second = rest.astype(jnp.bfloat16)
    third = (rest - second.astype(jnp.float32)).astype(jnp.bfloat16)
    parts[0:cols, :] = first
    parts[cols:2 * cols, :] = second
    parts[2 * cols:3 * cols, :] = third

    def block(step, carry):
        pieces = []
        for i in range(GROUP):
            value = (step * GROUP + i).astype(jnp.float32).astype(jnp.bfloat16)
            pieces.append(jnp.where(hib[...] == value, parts[...], jnp.bfloat16(0)))
        product = jnp.dot(jnp.concatenate(pieces, axis=0), onehot[...],
                          preferred_element_type=jnp.float32)
        for i in range(GROUP):
            base = i * 3 * cols
            piece = (product[base:base + cols] + product[base + cols:base + 2 * cols]) + product[base + 2 * cols:base + 3 * cols]
            at = pl.ds(pl.multiple_of((step * GROUP + i) * LOW, LOW), LOW)
            summed[:, at] = piece
            sq[:, at] = jnp.sum(piece * piece, axis=0, keepdims=True)
        return carry

    lax.fori_loop(0, total_rows // (LOW * GROUP), block, 0)

    def span_of(e):
        return pl.ds(pl.multiple_of(e * rows, rows), rows)

    def sq_copy(m, owner):
        return pltpu.make_async_remote_copy(
            src_ref=sq.at[:, span_of(d ^ m)], dst_ref=rs.at[owner],
            send_sem=q_send.at[m], recv_sem=q_recv.at[owner],
            device_id=(k, d ^ m), device_id_type=MESH)

    for m in range(nc - 1, 0, -1):
        sq_copy(m, d).start()
    tb[:, span_of(d)] = xt[pl.ds(pl.multiple_of(d * cols, cols), cols), :]
    total = sq[:, span_of(d)]
    for m in range(1, nc):
        sq_copy(m, d ^ m).wait_recv()
        total = total + rs[d ^ m]
    stbuf[:, span_of(d)] = state[...] + total / width

    def state_copy(m, owner):
        return pltpu.make_async_remote_copy(
            src_ref=stbuf.at[:, span_of(d)], dst_ref=stbuf.at[:, span_of(owner)],
            send_sem=s_send.at[m], recv_sem=s_recv.at[owner],
            device_id=(k, d ^ m), device_id_type=MESH)

    for m in range(nc - 1, 0, -1):
        state_copy(m, d).start()

    def finish(m):
        e = d ^ m
        at = span_of(e)
        if m:
            state_copy(m, e).wait_recv()
        scale = learn_rate / (jnp.sqrt(stbuf[:, at]) + epsilon)
        if m:
            for c in range(CHUNKS):
                table_copy(m, c, e).wait_recv()
        summed[:, at] = tb[:, at] - summed[:, at] * scale
        pltpu.make_async_copy(summed.at[:, at], out.at[0, :, at], o_sem.at[m]).start()

    order = [0, 1] + near + far[::-1]
    for m in order:
        finish(m)
    state_out[...] = stbuf[...]
    for m in range(1, ns):
        grad_copy(m, k).wait_send()
    for m in range(1, nc):
        for c in range(CHUNKS):
            table_copy(m, c, d).wait_send()
        sq_copy(m, d).wait_send()
        state_copy(m, d).wait_send()
    for m in order:
        at = span_of(d ^ m)
        pltpu.make_async_copy(summed.at[:, at], out.at[0, :, at], o_sem.at[m]).wait()


def solution(mesh):
    ns, nc = mesh.shape["src"], mesh.shape["col"]

    def body(saved_tables, saved_state, slot_table, row_ids, grads):
        _, rows, width = saved_tables.shape
        _, cols, upd = grads.shape
        total_rows = rows * nc
        f32, bf16 = jnp.float32, jnp.bfloat16
        vmem = pl.BlockSpec(memory_space=pltpu.VMEM)
        hbm = pl.BlockSpec(memory_space=pl.ANY)
        dma = pltpu.SemaphoreType.DMA
        return pl.pallas_call(
            functools.partial(kernel, ns, nc),
            out_shape=(jax.ShapeDtypeStruct((1, cols, total_rows), f32),
                       jax.ShapeDtypeStruct((1, total_rows), f32)),
            in_specs=[hbm, vmem, pl.BlockSpec(memory_space=pltpu.SMEM), vmem, hbm],
            out_specs=(hbm, vmem),
            scratch_shapes=[
                pltpu.VMEM((rows, width), f32),
                pltpu.VMEM((width, rows), f32),
                pltpu.VMEM((cols, total_rows), f32),
                pltpu.VMEM((cols, total_rows), f32),
                pltpu.VMEM((ns, cols, upd), f32),
                pltpu.VMEM((3 * cols, upd), bf16),
                pltpu.VMEM((3 * cols, upd), bf16),
                pltpu.VMEM((upd, LOW), bf16),
                pltpu.VMEM((1, total_rows), f32),
                pltpu.VMEM((nc, 1, rows), f32),
                pltpu.VMEM((1, total_rows), f32),
                dma((CHUNKS,)), dma(()), dma((ns,)), dma((ns,)),
                dma((nc, CHUNKS)), dma((nc, CHUNKS)),
                dma((nc,)), dma((nc,)), dma((nc,)), dma((nc,)), dma((nc,)),
            ],
            compiler_params=pltpu.CompilerParams(collective_id=0, has_side_effects=True),
        )(saved_tables, saved_state, slot_table, row_ids, grads)

    return jax.shard_map(
        body,
        mesh=mesh,
        in_specs=(P("src", "col", None), P("src", "col"), P(), P(), P("src", "col", None)),
        out_specs=(P("src", "col", None), P("src", None)),
        check_vma=False,
    )
```

time: 162 us -> 65.9 us (0.41)
  waiting for transfers between devices: 68.1 us -> 0 us
  Pallas kernels: 0 us -> 61.4 us
  other arithmetic: 36 us -> 0 us
  local copies, waits for them, and re-layouts: 21.3 us -> 3.71 us
  between operations: 16 us -> 0.65 us
  blocking collectives: 14 us -> 0 us
  starting transfers between devices: 6.43 us -> 0 us
    pallas_call x0 -> x1, Pallas kernels: none -> 61.4 us  [body(): pl.pallas_call(functools.partial(kernel, ns, nc), out_shape=(jax.ShapeDty...]
    psum x1 -> x0, waiting for transfers between devices: 40.8 us -> none  [target_update(): total = lax.psum(partial_value, 'col')]
    all_gather x1 -> x0, waiting for transfers between devices: 26.5 us -> none  [target_update(): every_grad = lax.all_gather(grads, 'src', axis=0, tiled=True)]
    scatter-add x1 -> x0, other arithmetic: 15.2 us -> none  [target_update(): jnp.zeros((length, slot_grad.shape[0]), jnp.float32).at[slot_ids]]
    all_gather x1 -> x0, blocking collectives: 14 us -> none  [reshard(): state_full = lax.all_gather(state, 'col', axis=1, tiled=True)]
    sub x1 -> x0, other arithmetic: 13.3 us -> none  [target_update(): tables[0] - learn_rate * summed / (jnp.sqrt(new_state)[:, None] + epsilon)]
    unnamed x7 -> x4, local copies, waits for them, and re-layouts: 14.8 us -> 3.71 us
    all_to_all x1 -> x0, starting transfers between devices: 6.35 us -> none  [reshard(): lax.all_to_all(tables, 'col', split_axis=2, concat_axis=1, tiled=True)]
  transfers between devices with their start and end apart: 3 -> 0, of which waited for: 2 -> 0; matrix products, arithmetic and copies ran while one was open for 15% -> 0% of each run, Pallas kernels for 0% -> 0%
where the time goes in v1:
time: 65.9 us; the launch traced here: 65.7 us
  Pallas kernels  61.4 us (93%)
  local copies, waits for them, and re-layouts  3.71 us (6%)
    pallas_call x1, Pallas kernels, body(): pl.pallas_call(functools.partial(kernel, ns, nc), out_shape=(jax.ShapeDty...  61.4 us
    unnamed x4, local copies, waits for them, and re-layouts  3.71 us

profile of v1, /device:TPU:0, one launch (start us, length us, event | category | flops | bytes accessed | tf_op | source)
XLA Modules:
  0.0 65.7 jit_solution(5904998744678943390)
XLA Ops:
  0.6 61.4 %shard_map.68 = (f32[1,32,16384]{2,1,0:T(8,128)}, f32[1,16384]{1,0:T(1,128)}) custom-call(f32[1,2048,256]{2,1,0:T(8,128)} %tab.1, f32[1,2048]{1,0:T(1,128)} %state.1, s32[4]{0:T(128)} %slot_table.1, s32[4,2048]{1,0:T(4,128)} %ids.1, f32[1,32,2048]{2,1,0:T(8,128)} %grads.1), custom_call_target="tpu_custom_call" | custom-call | tf_op jit(solution)/shard_map/pallas_call | solution.py:201
  62.0 0.0 copy-start
  62.0 3.1 %copy.9 = f32[1,32,16384]{2,1,0:T(8,128)} copy(f32[1,32,16384]{2,1,0:T(8,128)} %get-tuple-element.4) | data formatting | bytes 4194304
  65.1 0.0 copy-done
  65.1 0.6 copy.10
Async XLA Ops:
  62.0 3.1 %copy-start = (f32[1,16384]{1,0:T(1,128)S(1)}, f32[1,16384]{1,0:T(1,128)}, u32[]{:S(2)}) copy-start(f32[1,16384]{1,0:T(1,128)} %get-tuple-element.5) | copy-start | bytes 196612

commit v2 on v1

--- a/solution.py
+++ b/solution.py
@@ -14,13 +14,16 @@
 LANES = 128
 LOW = 256
 GROUP = 4
+VMEM_LIMIT = 50 << 20
 CHUNKS = 4
+EARLY = 2
+MIDDLE = 1
 
 
 def kernel(ns, nc, tab, state, slot_table, ids, grads, out, state_out,
            x, xt, tb, summed, gbuf, parts, hib, onehot, sq, rs, stbuf,
            x_sem, g_sem, gs_send, gs_recv, t_send, t_recv,
-           q_send, q_recv, s_send, s_recv, o_sem):
+           q_send, q_recv, s_send, s_recv):
     k = lax.axis_index("src")
     d = lax.axis_index("col")
     rows, width = x.shape
@@ -43,7 +46,6 @@
         pl.semaphore_signal(barrier, inc=1, device_id=(k, d ^ m), device_id_type=MESH)
     for m in range(1, ns):
         pl.semaphore_signal(barrier, inc=1, device_id=(k ^ m, d), device_id_type=MESH)
-    pl.semaphore_wait(barrier, nc + ns - 2)
 
     def grad_copy(m, owner):
         return pltpu.make_async_remote_copy(
@@ -51,8 +53,6 @@
             send_sem=gs_send.at[m], recv_sem=gs_recv.at[owner],
             device_id=(k ^ m, d), device_id_type=MESH)
 
-    for m in range(1, ns):
-        grad_copy(m, k).start()
 
     def table_copy(m, c, owner):
         e = d ^ m
@@ -64,27 +64,26 @@
 
     own_half = d // per
     near = list(range(per - 1, 1, -1))
-    far = list(range(nc - 1, per - 1, -1))
+    far = list(range(per, nc))
 
     def turn(half, c):
         at = pl.ds(pl.multiple_of(half * LANES, LANES), LANES)
         xt[at, pl.ds(c * ch, ch)] = x[pl.ds(c * ch, ch), at].T
 
-    queue = []
     for c in range(CHUNKS):
         loads[c].wait()
-        turn(own_half, c)
-        for m in queue:
-            table_copy(m, c - 1, d).start()
-        queue = near
-    for c in range(CHUNKS):
         for h in range(1, width // LANES):
             turn(own_half ^ h, c)
-        if c == 0:
+    pl.semaphore_wait(barrier, nc + ns - 2)
+    for c in range(EARLY):
+        for m in far:
+            table_copy(m, c, d).start()
+    for m in range(1, ns):
+        grad_copy(m, k).start()
+    for c in range(CHUNKS):
+        turn(own_half, c)
+        if c:
             for m in near:
-                table_copy(m, CHUNKS - 1, d).start()
-        else:
-            for m in far:
                 table_copy(m, c - 1, d).start()
 
     t = slot_table[k]
@@ -96,7 +95,7 @@
         for w in range(LOW // LANES):
             onehot[b * LANES:(b + 1) * LANES, w * LANES:(w + 1) * LANES] = jnp.where(
                 column == lane + float(w * LANES), 1.0, 0.0).astype(jnp.bfloat16)
-    for m in far:
+    for m in near:
         table_copy(m, CHUNKS - 1, d).start()
     for c in range(CHUNKS):
         table_copy(1, c, d).start()
@@ -143,6 +142,9 @@
 
     for m in range(nc - 1, 0, -1):
         sq_copy(m, d).start()
+    for c in range(EARLY, EARLY + MIDDLE):
+        for m in far:
+            table_copy(m, c, d).start()
     tb[:, span_of(d)] = xt[pl.ds(pl.multiple_of(d * cols, cols), cols), :]
     total = sq[:, span_of(d)]
     for m in range(1, nc):
@@ -158,6 +160,9 @@
 
     for m in range(nc - 1, 0, -1):
         state_copy(m, d).start()
+    for c in range(EARLY + MIDDLE, CHUNKS):
+        for m in far:
+            table_copy(m, c, d).start()
 
     def finish(m):
         e = d ^ m
@@ -168,10 +173,9 @@
         if m:
             for c in range(CHUNKS):
                 table_copy(m, c, e).wait_recv()
-        summed[:, at] = tb[:, at] - summed[:, at] * scale
-        pltpu.make_async_copy(summed.at[:, at], out.at[0, :, at], o_sem.at[m]).start()
-
-    order = [0, 1] + near + far[::-1]
+        out[0, :, at] = tb[:, at] - summed[:, at] * scale
+
+    order = [0, 1] + near + far
     for m in order:
         finish(m)
     state_out[...] = stbuf[...]
@@ -182,9 +186,6 @@
             table_copy(m, c, d).wait_send()
         sq_copy(m, d).wait_send()
         state_copy(m, d).wait_send()
-    for m in order:
-        at = span_of(d ^ m)
-        pltpu.make_async_copy(summed.at[:, at], out.at[0, :, at], o_sem.at[m]).wait()
 
 
 def solution(mesh):
@@ -203,7 +204,7 @@
             out_shape=(jax.ShapeDtypeStruct((1, cols, total_rows), f32),
                        jax.ShapeDtypeStruct((1, total_rows), f32)),
             in_specs=[hbm, vmem, pl.BlockSpec(memory_space=pltpu.SMEM), vmem, hbm],
-            out_specs=(hbm, vmem),
+            out_specs=(vmem, vmem),
             scratch_shapes=[
                 pltpu.VMEM((rows, width), f32),
                 pltpu.VMEM((width, rows), f32),
@@ -218,9 +219,9 @@
                 pltpu.VMEM((1, total_rows), f32),
                 dma((CHUNKS,)), dma(()), dma((ns,)), dma((ns,)),
                 dma((nc, CHUNKS)), dma((nc, CHUNKS)),
-                dma((nc,)), dma((nc,)), dma((nc,)), dma((nc,)), dma((nc,)),
+                dma((nc,)), dma((nc,)), dma((nc,)), dma((nc,)),
             ],
-            compiler_params=pltpu.CompilerParams(collective_id=0, has_side_effects=True),
+            compiler_params=pltpu.CompilerParams(collective_id=0, vmem_limit_bytes=VMEM_LIMIT, has_side_effects=True),
         )(saved_tables, saved_state, slot_table, row_ids, grads)
 
     return jax.shard_map(

time: 65.9 us -> 61.5 us (0.933); the launches traced: 65.7 us -> 60.4 us
  Pallas kernels: 61.4 us -> 54.8 us
  local copies, waits for them, and re-layouts: 3.71 us -> 5 us
    pallas_call x1, Pallas kernels: 61.4 us -> 54.8 us  [body(): pl.pallas_call(functools.partial(kernel, ns, nc), out_shape=(jax.ShapeDty...]
    unnamed x4 -> x10, local copies, waits for them, and re-layouts: 3.71 us -> 5 us
where the time goes in v2:
time: 61.5 us; the launch traced here: 60.4 us
  Pallas kernels  54.8 us (89%)
  local copies, waits for them, and re-layouts  5 us (8%)
  between operations  0.65 us (1%)
    pallas_call x1, Pallas kernels, body(): pl.pallas_call(functools.partial(kernel, ns, nc), out_shape=(jax.ShapeDty...  54.8 us
    unnamed x10, local copies, waits for them, and re-layouts  5 us

profile of v2, /device:TPU:0, one launch (start us, length us, event | category | flops | bytes accessed | tf_op | source)
XLA Modules:
  0.0 60.4 jit_solution(4288595531055038523)
XLA Ops:
  0.6 0.0 copy-start
  0.6 0.9 %copy-done = f32[1,32,2048]{2,1,0:T(8,128)S(1)} copy-done((f32[1,32,2048]{2,1,0:T(8,128)S(1)}, f32[1,32,2048]{2,1,0:T(8,128)}, u32[]{:S(2)}) %copy-start) | copy-done | bytes 262168
  1.6 0.0 copy-start.1
  1.6 0.8 %copy-done.1 = s32[4,2048]{1,0:T(4,128)S(1)} copy-done((s32[4,2048]{1,0:T(4,128)S(1)}, s32[4,2048]{1,0:T(4,128)}, u32[]{:S(2)}) %copy-start.1) | copy-done | bytes 32792
  2.3 0.0 copy-start.2
  2.3 0.7 %copy-done.2 = f32[1,2048]{1,0:T(1,128)S(1)} copy-done((f32[1,2048]{1,0:T(1,128)S(1)}, f32[1,2048]{1,0:T(1,128)}, u32[]{:S(2)}) %copy-start.2) | copy-done | bytes 8216
  3.0 0.0 copy-start.3
  3.0 0.7 %copy-done.3 = s32[4]{0:T(128)S(1)} copy-done((s32[4]{0:T(128)S(1)}, s32[4]{0:T(128)}, u32[]{:S(2)}) %copy-start.3) | copy-done | bytes 40
  3.7 54.8 %shard_map.68 = (f32[1,32,16384]{2,1,0:T(8,128)S(1)}, f32[1,16384]{1,0:T(1,128)S(1)}) custom-call(f32[1,2048,256]{2,1,0:T(8,128)} %tab.1, f32[1,2048]{1,0:T(1,128)S(1)} %copy-done.2, s32[4]{0:T(128)S(1)} %copy-done.3, s32[4,2048]{1,0:T(4,128)S(1)} %copy-done.1, f32[1,32,2048]{2,1,0:T(8,128)S(1)} %copy-done), custom_call_target="tpu_custom_call" | custom-call | tf_op jit(solution)/shard_map/pallas_call | solution.py:202
  58.5 1.3 %copy.9 = f32[1,32,16384]{2,1,0:T(8,128)} copy(f32[1,32,16384]{2,1,0:T(8,128)S(1)} %get-tuple-element.4) | data formatting | bytes 4194304
  59.8 0.6 %copy.10 = f32[1,16384]{1,0:T(1,128)} copy(f32[1,16384]{1,0:T(1,128)S(1)} %get-tuple-element.5) | data formatting | bytes 131072
Async XLA Ops:
  0.6 1.0 %copy-start = (f32[1,32,2048]{2,1,0:T(8,128)S(1)}, f32[1,32,2048]{2,1,0:T(8,128)}, u32[]{:S(2)}) copy-start(f32[1,32,2048]{2,1,0:T(8,128)} %grads.1) | copy-start | bytes 786436
  1.6 0.8 %copy-start.1 = (s32[4,2048]{1,0:T(4,128)S(1)}, s32[4,2048]{1,0:T(4,128)}, u32[]{:S(2)}) copy-start(s32[4,2048]{1,0:T(4,128)} %ids.1) | copy-start | bytes 98308
  2.3 0.7 %copy-start.2 = (f32[1,2048]{1,0:T(1,128)S(1)}, f32[1,2048]{1,0:T(1,128)}, u32[]{:S(2)}) copy-start(f32[1,2048]{1,0:T(1,128)} %state.1) | copy-start | bytes 24580
  3.0 0.7 %copy-start.3 = (s32[4]{0:T(128)S(1)}, s32[4]{0:T(128)}, u32[]{:S(2)}) copy-start(s32[4]{0:T(128)} %slot_table.1) | copy-start | bytes 52

commit v3 on v2

--- a/solution.py
+++ b/solution.py
@@ -13,7 +13,7 @@
 MESH = pl.DeviceIdType.MESH
 LANES = 128
 LOW = 256
-GROUP = 4
+GROUP = 8
 VMEM_LIMIT = 50 << 20
 CHUNKS = 4
 EARLY = 2
@@ -129,7 +129,6 @@
             sq[:, at] = jnp.sum(piece * piece, axis=0, keepdims=True)
         return carry
 
-    lax.fori_loop(0, total_rows // (LOW * GROUP), block, 0)
 
     def span_of(e):
         return pl.ds(pl.multiple_of(e * rows, rows), rows)
@@ -140,8 +139,14 @@
             send_sem=q_send.at[m], recv_sem=q_recv.at[owner],
             device_id=(k, d ^ m), device_id_type=MESH)
 
-    for m in range(nc - 1, 0, -1):
-        sq_copy(m, d).start()
+    steps = rows // (LOW * GROUP)
+    ready = None
+    for m in far + near + [1, 0]:
+        base = (d ^ m) * steps
+        lax.fori_loop(base, base + steps, block, 0)
+        if ready is not None:
+            sq_copy(ready, d).start()
+        ready = m
     for c in range(EARLY, EARLY + MIDDLE):
         for m in far:
             table_copy(m, c, d).start()

time: 61.5 us -> 60.1 us (0.977)
  Pallas kernels: 54.8 us -> 53.5 us
    pallas_call x1, Pallas kernels: 54.8 us -> 53.5 us  [body(): pl.pallas_call(functools.partial(kernel, ns, nc), out_shape=(jax.ShapeDty...]
where the time goes in v3:
time: 60.1 us; the launch traced here: 59.1 us
  Pallas kernels  53.5 us (89%)
  local copies, waits for them, and re-layouts  5 us (8%)
  between operations  0.65 us (1%)
    pallas_call x1, Pallas kernels, body(): pl.pallas_call(functools.partial(kernel, ns, nc), out_shape=(jax.ShapeDty...  53.5 us
    unnamed x10, local copies, waits for them, and re-layouts  5 us

profile of v3, /device:TPU:0, one launch (start us, length us, event | category | flops | bytes accessed | tf_op | source)
XLA Modules:
  0.0 59.1 jit_solution(3736906627803697930)
XLA Ops:
  0.6 0.0 copy-start
  0.6 0.9 %copy-done = f32[1,32,2048]{2,1,0:T(8,128)S(1)} copy-done((f32[1,32,2048]{2,1,0:T(8,128)S(1)}, f32[1,32,2048]{2,1,0:T(8,128)}, u32[]{:S(2)}) %copy-start) | copy-done | bytes 262168
  1.6 0.0 copy-start.1
  1.6 0.8 %copy-done.1 = s32[4,2048]{1,0:T(4,128)S(1)} copy-done((s32[4,2048]{1,0:T(4,128)S(1)}, s32[4,2048]{1,0:T(4,128)}, u32[]{:S(2)}) %copy-start.1) | copy-done | bytes 32792
  2.3 0.0 copy-start.2
  2.3 0.7 %copy-done.2 = f32[1,2048]{1,0:T(1,128)S(1)} copy-done((f32[1,2048]{1,0:T(1,128)S(1)}, f32[1,2048]{1,0:T(1,128)}, u32[]{:S(2)}) %copy-start.2) | copy-done | bytes 8216
  3.0 0.0 copy-start.3
  3.0 0.7 %copy-done.3 = s32[4]{0:T(128)S(1)} copy-done((s32[4]{0:T(128)S(1)}, s32[4]{0:T(128)}, u32[]{:S(2)}) %copy-start.3) | copy-done | bytes 40
  3.7 53.5 %shard_map.68 = (f32[1,32,16384]{2,1,0:T(8,128)S(1)}, f32[1,16384]{1,0:T(1,128)S(1)}) custom-call(f32[1,2048,256]{2,1,0:T(8,128)} %tab.1, f32[1,2048]{1,0:T(1,128)S(1)} %copy-done.2, s32[4]{0:T(128)S(1)} %copy-done.3, s32[4,2048]{1,0:T(4,128)S(1)} %copy-done.1, f32[1,32,2048]{2,1,0:T(8,128)S(1)} %copy-done), custom_call_target="tpu_custom_call" | custom-call | tf_op jit(solution)/shard_map/pallas_call | solution.py:207
  57.2 1.3 %copy.9 = f32[1,32,16384]{2,1,0:T(8,128)} copy(f32[1,32,16384]{2,1,0:T(8,128)S(1)} %get-tuple-element.4) | data formatting | bytes 4194304
  58.5 0.6 %copy.10 = f32[1,16384]{1,0:T(1,128)} copy(f32[1,16384]{1,0:T(1,128)S(1)} %get-tuple-element.5) | data formatting | bytes 131072
Async XLA Ops:
  0.6 1.0 %copy-start = (f32[1,32,2048]{2,1,0:T(8,128)S(1)}, f32[1,32,2048]{2,1,0:T(8,128)}, u32[]{:S(2)}) copy-start(f32[1,32,2048]{2,1,0:T(8,128)} %grads.1) | copy-start | bytes 786436
  1.6 0.8 %copy-start.1 = (s32[4,2048]{1,0:T(4,128)S(1)}, s32[4,2048]{1,0:T(4,128)}, u32[]{:S(2)}) copy-start(s32[4,2048]{1,0:T(4,128)} %ids.1) | copy-start | bytes 98308
  2.3 0.7 %copy-start.2 = (f32[1,2048]{1,0:T(1,128)S(1)}, f32[1,2048]{1,0:T(1,128)}, u32[]{:S(2)}) copy-start(f32[1,2048]{1,0:T(1,128)} %state.1) | copy-start | bytes 24580
  3.0 0.7 %copy-start.3 = (s32[4]{0:T(128)S(1)}, s32[4]{0:T(128)}, u32[]{:S(2)}) copy-start(s32[4]{0:T(128)} %slot_table.1) | copy-start | bytes 52
